TPU v7x, 32 devices: a whole 2x2x4 slice. The times are simulated.
32 devices in a mesh: pert: 2 (over x), ga: 16 (over z, y, core).
Axes of the slice: x: 2, y: 2, z: 4, core: 2. Of those that a mesh axis runs over, the one named last changes fastest.
Arguments:
- psi_k: bfloat16 [2, 8192, 256], P(None, 'ga'), may hold values from -6 to 6
- beta_k: bfloat16 [2, 8192, 2496], P(None, 'ga'), may hold values from -0.0625 to 0.0625
- beta_kq: bfloat16 [2, 8192, 2496], P(None, 'ga'), may hold values from -0.15625 to 0.15625
- g_k: float32 [3, 8192], P(None, 'ga'), may hold values from -2 to 2
- g_kq: float32 [3, 8192], P(None, 'ga'), may hold values from -2 to 2
- send_index: int32 [16, 16, 32], P('ga'), may hold values from -1 to 511, as said below
- recv_index: int32 [8192], P('ga'), may hold values from -1 to 511, as said below
- dmat: float32 [192, 13, 13], replicated, may hold values from -0.5 to 4, as said below
- displaced: int32 [256], P('pert'), parts along dimension 0, may hold values from 0 to 191, as said below
- mode: float32 [3, 256], P(None, 'pert'), parts along dimension 1, may hold values from -5 to 5
Outputs:
- dvpsi: bfloat16 [4, 8192, 256], P('pert', 'ga'), parts along dimension 0
There are 2 independent parts, one for each index of `pert`. A program takes and returns all parts, laid end to end along the dimension named above; an argument that names none is the same for every part. Nothing has to cross between parts.
Inputs may be any that keep to these rules, and one draw needn't show every extreme that they name: `send_index`: entry [s, d, c] is a row of device s's k-sphere block in local numbering, or -1 for an unused slot; the rows device s sends are distinct; in every draw some device receives 32 rows from every device. `recv_index`: entry r is s * 32 + c, naming slot c from device s among the rows received by the device of row r, or -1 for a row with no k-sphere counterpart; every used slot is named by exactly one row of its receiving device and no unused slot is named. `dmat`: each atom's block is symmetric. `displaced`: 128 distinct atoms.
All inputs are finite; a program needn't handle non-finite values.
Results may differ from a plain program's by a relative error of at most 0.0057.
Values may be sent and summed in bfloat16 or wider, within the bound.
A program may use at most 128 MiB of HBM per device.

v0:
```python
import functools

import jax
import jax.numpy as jnp
import numpy as np
from jax import lax
from jax.experimental import pallas as pl
from jax.experimental.pallas import tpu as pltpu
from jax.sharding import PartitionSpec as P

LANES = 128
RING = 4
CORE_Y = 4
BF16 = jnp.bfloat16
F32 = jnp.float32
VMEM_LIMIT = 56 * 1024 * 1024


def round_up(value, step):
    return -(-value // step) * step


def dot(a, b):
    return jnp.dot(a, b, preferred_element_type=F32)


def dot_t(a, b):
    return lax.dot_general(a, b, (((0,), (0,)), ((), ())), preferred_element_type=F32)


def pack_kernel(slot_ref, psi_ref, out_ref):
    rows = psi_ref.shape[1]
    bands = psi_ref.shape[2]
    slots = slot_ref.shape[1]
    pick = (lax.broadcasted_iota(jnp.int32, (rows, slots), 0) == slot_ref[...]).astype(BF16)
    for part in range(2):
        out_ref[:, part * bands:(part + 1) * bands] = dot_t(pick, psi_ref[part]).astype(BF16)


def pack_rows(slots, psi_k):
    return pl.pallas_call(
        pack_kernel,
        out_shape=jax.ShapeDtypeStruct((slots.shape[1], 2 * psi_k.shape[2]), BF16),
        compiler_params=pltpu.CompilerParams(vmem_limit_bytes=VMEM_LIMIT),
    )(slots, psi_k)


class Layout:
    def __init__(self, groups, atoms, per_atom, total):
        self.groups = groups
        self.blocks = groups // CORE_Y
        self.gang = CORE_Y
        if self.blocks != RING:
            self.blocks = RING
            self.gang = groups // RING
        self.per_shard = atoms // groups
        self.per_atom = per_atom
        self.used = self.per_shard * per_atom
        self.rows = round_up(self.used, 16)
        self.block = self.gang * self.rows
        self.padded = round_up(self.block, LANES)
        self.total = total
        slack = total - atoms * per_atom
        self.window = min(total, round_up(self.gang * self.used + slack + 16, LANES))
        self.starts = [
            min(b * self.gang * self.used // 16 * 16, total - self.window) for b in range(self.blocks)
        ]


def columns_of(layout, info_ref, b):
    wide = info_ref[:, b * layout.padded:(b + 1) * layout.padded]
    return jnp.transpose(wide)[: layout.block]


def select(layout, beta_ref, info, b):
    start = layout.starts[b]
    ids = lax.broadcasted_iota(jnp.int32, (layout.block, layout.window), 1) + start
    pick = (ids == info[:, 0:1].astype(jnp.int32)).astype(BF16)
    rows = pl.ds(start, layout.window)
    return dot(pick, beta_ref[0, rows, :]), dot(pick, beta_ref[1, rows, :])


def row_scale(g_ref, info):
    total = info[:, 1:2] * g_ref[0:1, :]
    for x in range(1, g_ref.shape[0]):
        total = total + info[:, x + 1:x + 2] * g_ref[x:x + 1, :]
    return total


def regroup(arrived_ref, slot_ref, wave):
    slots, rows = arrived_ref.shape[0], wave.shape[0]
    pick = (lax.broadcasted_iota(jnp.int32, (slots, rows), 0) == slot_ref[...]).astype(BF16)
    wave[...] = dot_t(pick, arrived_ref[...]).astype(BF16)


def selected_terms(layout, beta_ref, info, g_ref, b):
    real, imag = select(layout, beta_ref, info, b)
    scale = row_scale(g_ref, info)
    return real, imag, scale * imag, scale * real


def project_block(terms, stacked, store):
    bands = stacked.shape[1] // 2
    x = dot(terms[0], stacked)
    y = dot(terms[1], stacked)
    store(0, (x[:, :bands] + y[:, bands:]).astype(BF16))
    store(1, (x[:, bands:] - y[:, :bands]).astype(BF16))
    x = dot(terms[2], stacked)
    y = dot(terms[3], stacked)
    store(2, (x[:, :bands] - y[:, bands:]).astype(BF16))
    store(3, (x[:, bands:] + y[:, :bands]).astype(BF16))


def prepare_block(layout, beta_ref, info, g_ref, left_ref, b):
    real, imag, slope_real, slope_imag = selected_terms(layout, beta_ref, info, g_ref, b)
    for k, term in enumerate((slope_real, -slope_imag, real, imag)):
        left_ref[b, k] = term.astype(BF16).T


def back_block(left_ref, b, coupled):
    width = coupled.shape[1] // 2
    bands = width // 2
    first, second = coupled[:, :width], coupled[:, width:]
    x = dot(left_ref[b, 0], first) + dot(left_ref[b, 2], second)
    y = dot(left_ref[b, 1], first) + dot(left_ref[b, 3], second)
    return x[:, :bands] - y[:, bands:], x[:, bands:] + y[:, :bands]


def project_kernel(layout, arrived_ref, slot_ref, beta_ref, info_ref, g_ref, out_ref, wave):
    regroup(arrived_ref, slot_ref, wave)
    bands = wave.shape[1] // 2
    for b in range(layout.blocks):

        def store(k, value, b=b):
            out_ref[b * layout.block:(b + 1) * layout.block, k * bands:(k + 1) * bands] = value

        info = columns_of(layout, info_ref, b)
        terms = [term.astype(BF16) for term in selected_terms(layout, beta_ref, info, g_ref, b)]
        project_block(terms, wave[...], store)


def finish_kernel(layout, beta_ref, info_ref, g_ref, coupled_ref, out_ref, left, total):
    for b in range(layout.blocks):
        prepare_block(layout, beta_ref, columns_of(layout, info_ref, b), g_ref, left, b)
        parts = back_block(left, b, coupled_ref[b * layout.block:(b + 1) * layout.block, :])
        for k in range(2):
            total[k] = parts[k] if b == 0 else total[k] + parts[k]
    out_ref[...] = total[...].astype(BF16)


def params(**extra):
    return pltpu.CompilerParams(vmem_limit_bytes=VMEM_LIMIT, **extra)


def separate_steps(layout, arrived, slots, beta_k, beta_kq, info, g_k, g_kq, coupling):
    rows, width = slots.shape[1], arrived.shape[1]
    terms = pl.pallas_call(
        functools.partial(project_kernel, layout),
        out_shape=jax.ShapeDtypeStruct((layout.groups * layout.rows, 2 * width), BF16),
        scratch_shapes=[pltpu.VMEM((rows, width), BF16)],
        compiler_params=params(),
    )(arrived, slots, beta_k, info, g_k)
    shard = lax.psum_scatter(terms.astype(F32), "ga", scatter_dimension=0, tiled=True)
    mixed = jnp.dot(
        coupling, shard, precision=lax.Precision.HIGHEST, preferred_element_type=F32
    ).astype(BF16)
    coupled = lax.all_gather(mixed, "ga", axis=0, tiled=True)
    return pl.pallas_call(
        functools.partial(finish_kernel, layout),
        out_shape=jax.ShapeDtypeStruct((2, rows, width // 2), BF16),
        scratch_shapes=[
            pltpu.VMEM((layout.blocks, 4, rows, layout.block), BF16),
            pltpu.VMEM((2, rows, width // 2), F32),
        ],
        compiler_params=params(),
    )(beta_kq, info, g_kq, coupled)


class Sends:
    def __init__(self, send_sem, recv_sem):
        self.send_sem, self.recv_sem = send_sem, recv_sem
        self.started = []

    def start(self, source, target, device):
        k = len(self.started)
        copy = pltpu.make_async_remote_copy(
            src_ref=source,
            dst_ref=target,
            send_sem=self.send_sem.at[k],
            recv_sem=self.recv_sem.at[k],
            device_id={"ga": device},
            device_id_type=pl.DeviceIdType.MESH,
        )
        copy.start()
        self.started.append(copy)
        return copy

    def finish(self):
        for copy in self.started:
            copy.wait_send()


def exact_dot(a, b):
    return jnp.dot(a, b, precision=lax.Precision.HIGHEST, preferred_element_type=F32)


def slot_row(send_ref):
    receivers, cap = send_ref.shape
    column = lax.broadcasted_iota(jnp.int32, (cap, receivers * cap), 1)
    inner = lax.broadcasted_iota(jnp.int32, (cap, receivers * cap), 0)
    wide = exact_dot(send_ref[...].astype(F32), (column % cap == inner).astype(F32))
    column = lax.broadcasted_iota(jnp.int32, wide.shape, 1)
    outer = lax.broadcasted_iota(jnp.int32, wide.shape, 0)
    return jnp.sum(jnp.where(column // cap == outer, wide, 0.0), axis=0, keepdims=True).astype(jnp.int32)


def sorted_info(layout, displaced_ref, mode_ref, table_ref, values, info):
    parts = mode_ref.shape[0]
    values[...] = jnp.zeros_like(values)
    values[0:1, :] = displaced_ref[...].astype(F32)
    values[1:1 + parts, :] = mode_ref[...]
    by_atom = jnp.transpose(values[...])
    smaller = (by_atom[:, 0:1] < values[0:1, :]).astype(F32)
    rank = jnp.sum(smaller, axis=0, keepdims=True)
    lane = lax.broadcasted_iota(jnp.int32, (layout.block, values.shape[0]), 1)
    for b in range(layout.blocks):
        place = columns_of(layout, table_ref, b)
        found = exact_dot((place[:, 0:1] == rank).astype(F32), by_atom)
        source = jnp.where(place[:, 0:1] < 0, -1.0, found * layout.per_atom + place[:, 1:2])
        info[b] = jnp.where(lane == 0, source, jnp.where(lane == 7, found[:, 0:1], found))


def coupling_matrix(layout, dmat_ref, atom, proj, spread_ref, same_ref):
    lanes = lax.broadcasted_iota(jnp.int32, (layout.rows, dmat_ref.shape[2]), 1)
    pick = (lanes == atom.astype(jnp.int32)).astype(F32)
    rows = jnp.zeros((layout.rows, layout.per_atom), F32)
    for i in range(layout.per_atom):
        found = lax.dot_general(
            pick, dmat_ref[i], (((1,), (1,)), ((), ())),
            precision=lax.Precision.HIGHEST, preferred_element_type=F32,
        )
        rows = rows + jnp.where(proj == i, found, 0.0)
    return exact_dot(rows, spread_ref[...]) * same_ref[...]


def fused_kernel(
    layout, psi_ref, send_ref, slot_ref, displaced_ref, mode_ref, table_ref, g_k_ref, g_kq_ref, dmat_ref,
    proj_ref, spread_ref, same_ref, beta_k_hbm, beta_kq_hbm,
    out_ref, wave, part, core_in, mine, y_in, y_sum, za_in, za_mid, zb_in, zb_mid, b_sum, b_in,
    coupled, left, total, beta_kq, beta_k, packed, arrived, terms, values, info, send_sem, recv_sem, load_sem,
):
    me = lax.axis_index("ga")
    n = layout.groups
    c, y, z = me % 2, (me // 2) % 2, me // 4

    def index(zz, yy, cc):
        return (zz * 2 + yy) * 2 + cc

    up, down, far = (z + 1) % RING, (z + RING - 1) % RING, (z + 2) % RING
    other_core, other_y = index(z, y, 1 - c), index(z, 1 - y, c)
    next_z, last_z = index(up, y, c), index(down, y, c)
    load_k = pltpu.make_async_copy(beta_k_hbm, beta_k, load_sem.at[0])
    load_k.start()
    load = pltpu.make_async_copy(beta_kq_hbm, beta_kq, load_sem.at[1])
    load.start()

    barrier = pltpu.get_barrier_semaphore()
    for step in range(1, n):
        pl.semaphore_signal(
            barrier, inc=1, device_id={"ga": (me + step) % n}, device_id_type=pl.DeviceIdType.MESH
        )
    rows_here, slots = psi_ref.shape[1], n * send_ref.shape[1]
    cap = send_ref.shape[1]
    pick = (lax.broadcasted_iota(jnp.int32, (rows_here, slots), 0) == slot_row(send_ref)).astype(BF16)
    for k in range(2):
        width = psi_ref.shape[2]
        packed[:, :, k * width:(k + 1) * width] = dot_t(pick, psi_ref[k]).astype(BF16).reshape(n, cap, width)
    pl.semaphore_wait(barrier, n - 1)

    sends = Sends(send_sem, recv_sem)
    rows = layout.rows
    bands = wave.shape[1] // 2
    half = 2 * bands
    low, high = pl.ds(0, half), pl.ds(half, half)
    left_cols, right_cols = pl.ds(0, bands), pl.ds(bands, bands)
    high_left, high_right = pl.ds(half, bands), pl.ds(half + bands, bands)

    def add(first, *others):
        value = first.astype(F32)
        for other in others:
            value = value + other.astype(F32)
        return value

    psi_copies = [
        sends.start(packed.at[(me + step) % n], arrived.at[me], (me + step) % n) for step in far_first(n)
    ]
    arrived[me] = packed[me]
    sorted_info(layout, displaced_ref, mode_ref, table_ref, values, info)
    load_k.wait()
    for b in range(RING):
        for k, term in enumerate(selected_terms(layout, beta_k, info[b], g_k_ref, b)):
            terms[b, k] = term.astype(BF16)
    load.wait()
    prepare_block(layout, beta_kq, info[0], g_kq_ref, left, 0)
    for copy in psi_copies:
        copy.wait_recv()

    pick = (lax.broadcasted_iota(jnp.int32, (slots, rows_here), 0) == slot_ref[...]).astype(BF16)
    wave[...] = dot_t(pick, arrived[...].reshape(slots, 2 * bands)).astype(BF16)
    order = (far, up, down, z)
    core_copies, y_copies, z_copies = [], [], []

    def settle(i):
        b = order[i]
        for yy in range(2):
            core_copies[i][yy].wait_recv()
            mine[b, yy] = add(part[b, yy, c], core_in[b, yy]).astype(BF16)
        if i == 0:
            z_copies.append(sends.start(mine.at[b, :, :, high_left], zb_in.at[0], next_z))
            z_copies.append(sends.start(mine.at[b, :, :, high_right], zb_in.at[1], last_z))
        if i == 1:
            z_copies.append(sends.start(mine.at[b, :, :, high_right], zb_in.at[2], next_z))
        if i == 2:
            z_copies.append(sends.start(mine.at[b, :, :, high_left], zb_in.at[3], last_z))
        y_copies.append(sends.start(mine.at[b, 1 - y, :, low], y_in.at[b], other_y))

    for i, b in enumerate(order):

        def store(k, value, b=b):
            for yy in range(2):
                for cc in range(2):
                    at = (yy * 2 + cc) * rows
                    part[b, yy, cc, :, k * bands:(k + 1) * bands] = value[at:at + rows]

        project_block([terms[b, k] for k in range(4)], wave[...], store)
        core_copies.append([
            sends.start(part.at[b, yy, 1 - c], core_in.at[b, yy], other_core) for yy in range(2)
        ])
        if i > 0:
            settle(i - 1)
    settle(RING - 1)
    zb_up, zb_down, zb_up_own, zb_down_own = z_copies

    def y_settle(i):
        b = order[i]
        y_copies[i].wait_recv()
        y_sum[b] = add(mine[b, y, :, :half], y_in[b]).astype(BF16)

    shard_atom = info[z, pl.ds(pl.multiple_of((y * 2 + c) * rows, 8), rows), 7:8]
    coupling = coupling_matrix(layout, dmat_ref, shard_atom, proj_ref[...], spread_ref, same_ref)
    zb_up.wait_recv()
    zb_mid[0] = add(mine[up, :, :, half:half + bands], zb_in[0]).astype(BF16)
    zb_up_sum = sends.start(zb_mid.at[0], zb_in.at[4], next_z)
    zb_down.wait_recv()
    zb_mid[1] = add(mine[down, :, :, half + bands:], zb_in[1]).astype(BF16)
    zb_down_sum = sends.start(zb_mid.at[1], zb_in.at[5], last_z)

    y_settle(0)
    za_up = sends.start(y_sum.at[far, :, left_cols], za_in.at[0], next_z)
    za_down = sends.start(y_sum.at[far, :, right_cols], za_in.at[1], last_z)
    prepare_block(layout, beta_kq, info[1], g_kq_ref, left, 1)
    y_settle(1)
    za_up_own = sends.start(y_sum.at[up, :, right_cols], za_in.at[2], next_z)
    y_settle(2)
    za_down_own = sends.start(y_sum.at[down, :, left_cols], za_in.at[3], last_z)
    prepare_block(layout, beta_kq, info[2], g_kq_ref, left, 2)

    for copy in (zb_up_own, zb_down_own, zb_up_sum, zb_down_sum):
        copy.wait_recv()
    b_sum[:, :, :bands] = add(mine[z, :, :, half:half + bands], zb_in[4], zb_in[3]).astype(BF16)
    b_sum[:, :, bands:] = add(mine[z, :, :, half + bands:], zb_in[5], zb_in[2]).astype(BF16)
    b_y = sends.start(b_sum.at[1 - y], b_in, other_y)

    za_up.wait_recv()
    za_mid[0] = add(y_sum[up, :, :bands], za_in[0]).astype(BF16)
    za_up_sum = sends.start(za_mid.at[0], za_in.at[4], next_z)
    za_down.wait_recv()
    za_mid[1] = add(y_sum[down, :, bands:], za_in[1]).astype(BF16)
    za_down_sum = sends.start(za_mid.at[1], za_in.at[5], last_z)
    y_settle(3)

    prepare_block(layout, beta_kq, info[3], g_kq_ref, left, 3)

    def couple(value):
        return exact_dot(coupling, value).astype(BF16)

    b_y.wait_recv()
    coupled[z, y, c, :, half:] = couple(add(b_sum[y], b_in[...]))
    own = coupled.at[z, y, c, :, high]
    gb_y = sends.start(own, own, other_y)
    for copy in (za_up_own, za_down_own, za_up_sum, za_down_sum):
        copy.wait_recv()
    coupled[z, y, c, :, :bands] = couple(add(y_sum[z, :, :bands], za_in[4], za_in[3]))
    coupled[z, y, c, :, bands:half] = couple(add(y_sum[z, :, bands:], za_in[5], za_in[2]))

    own = coupled.at[z, y, c, :, low]
    ga_up = sends.start(own, own, next_z)
    ga_down = sends.start(own, own, last_z)
    ga_y = [sends.start(own, own, other_y)]
    gc = [sends.start(coupled.at[z, y, c], coupled.at[z, y, c], other_core)]
    gb_y.wait_recv()
    pair = coupled.at[z, :, c, :, high]
    gb_up = sends.start(pair, pair, next_z)
    gb_down = sends.start(pair, pair, last_z)

    def forward(ref, device):
        return sends.start(ref, ref, device)

    ga_up.wait_recv()
    from_down_a = coupled.at[down, y, c, :, low]
    ga_up2 = forward(coupled.at[down, y, c, :, left_cols], next_z)
    ga_y.append(forward(from_down_a, other_y))
    ga_down.wait_recv()
    from_up_a = coupled.at[up, y, c, :, low]
    ga_down2 = forward(coupled.at[up, y, c, :, right_cols], last_z)
    ga_y.append(forward(from_up_a, other_y))
    ga_y[0].wait_recv()
    gc.append(forward(coupled.at[z, 1 - y, c], other_core))

    gb_up.wait_recv()
    gb_up2 = forward(coupled.at[down, :, c, :, high_left], next_z)
    gc_down = forward(coupled.at[down, :, c, :, high], other_core)
    gb_down.wait_recv()
    gb_down2 = forward(coupled.at[up, :, c, :, high_right], last_z)
    gc_up = forward(coupled.at[up, :, c, :, high], other_core)

    def back(b, first):
        parts = back_block(left, b, coupled[b].reshape(layout.block, 2 * half))
        for k in range(2):
            total[k] = parts[k] if first else total[k] + parts[k]

    for copy in gc:
        copy.wait_recv()
    back(z, True)

    ga_up2.wait_recv()
    ga_down2.wait_recv()
    ga_y.append(forward(coupled.at[far, y, c, :, low], other_y))
    ga_y[1].wait_recv()
    gc_down_a = forward(coupled.at[down, :, c, :, low], other_core)
    ga_y[2].wait_recv()
    gc_up_a = forward(coupled.at[up, :, c, :, low], other_core)
    gc_down.wait_recv()
    gc_down_a.wait_recv()
    back(down, False)
    gb_up2.wait_recv()
    gb_down2.wait_recv()
    gc_far = forward(coupled.at[far, :, c, :, high], other_core)
    ga_y[3].wait_recv()
    gc_far_a = forward(coupled.at[far, :, c, :, low], other_core)
    gc_up.wait_recv()
    gc_up_a.wait_recv()
    back(up, False)
    gc_far.wait_recv()
    gc_far_a.wait_recv()
    parts = back_block(left, far, coupled[far].reshape(layout.block, 2 * half))
    for k in range(2):
        out_ref[k] = (total[k] + parts[k]).astype(BF16)
    sends.finish()


COPIES = 80


def far_first(n):
    return sorted(range(1, n), key=lambda step: -min(step, n - step))


def tables(layout):
    row = np.arange(layout.rows)
    valid = row < layout.used
    slot = np.where(valid, row // layout.per_atom, 0)
    proj = np.where(valid, row % layout.per_atom, -1)
    table = np.zeros((8, layout.blocks, layout.padded), np.float32)
    table[0] = -1.0
    for b in range(layout.blocks):
        for k in range(layout.gang):
            at = slice(k * layout.rows, (k + 1) * layout.rows)
            table[0, b, at] = np.where(valid, (b * layout.gang + k) * layout.per_shard + slot, -1)
            table[1, b, at] = np.where(valid, proj, 0)
    spread = (np.arange(layout.per_atom)[:, None] == proj[None]).astype(np.float32)
    same = (slot[:, None] == slot[None]) & valid[:, None] & valid[None]
    return (
        table.reshape(8, -1),
        proj[:, None].astype(np.int32),
        spread,
        same.astype(np.float32),
    )


def fused(layout, psi_k, send_index, recv_index, beta_k, beta_kq, displaced, mode, g_k, g_kq, dmat):
    rows, bands = psi_k.shape[1:]
    width = 2 * bands
    cap = send_index.shape[2]
    table, proj, spread, same = (jnp.asarray(value) for value in tables(layout))
    r = layout.rows
    vmem = pl.BlockSpec(memory_space=pltpu.VMEM)

    def buffer(*shape, dtype=BF16):
        return pltpu.VMEM(shape, dtype)

    return pl.pallas_call(
        functools.partial(fused_kernel, layout),
        in_specs=[vmem] * 12 + [pl.BlockSpec(memory_space=pl.ANY)] * 2,
        out_specs=vmem,
        out_shape=jax.ShapeDtypeStruct((2, rows, bands), BF16),
        scratch_shapes=[
            buffer(rows, width),
            buffer(RING, 2, 2, r, 2 * width),
            buffer(RING, 2, r, 2 * width),
            buffer(RING, 2, r, 2 * width),
            buffer(RING, r, width),
            buffer(RING, r, width),
            buffer(6, r, bands),
            buffer(2, r, bands),
            buffer(6, 2, r, bands),
            buffer(2, 2, r, bands),
            buffer(2, r, width),
            buffer(r, width),
            buffer(RING, 2, 2, r, 2 * width),
            buffer(RING, 4, rows, layout.block),
            buffer(2, rows, bands, dtype=F32),
            pltpu.VMEM(beta_kq.shape, BF16),
            pltpu.VMEM(beta_k.shape, BF16),
            buffer(layout.groups, cap, width),
            buffer(layout.groups, cap, width),
            buffer(RING, 4, layout.block, rows),
            buffer(8, displaced.shape[0], dtype=F32),
            buffer(RING, layout.block, 8, dtype=F32),
            pltpu.SemaphoreType.DMA((COPIES,)),
            pltpu.SemaphoreType.DMA((COPIES,)),
            pltpu.SemaphoreType.DMA((2,)),
        ],
        compiler_params=params(collective_id=0, has_side_effects=True),
    )(
        psi_k, send_index[0], recv_index.reshape(1, -1), displaced.reshape(1, -1), mode, table, g_k, g_kq,
        jnp.transpose(dmat, (1, 2, 0)), proj, spread, same, beta_k, beta_kq,
    )


def pad_rows(layout, values, fill):
    k = values.shape[0]
    parts = values.reshape(k, layout.groups, layout.used)
    parts = jnp.pad(parts, ((0, 0), (0, 0), (0, layout.rows - layout.used)), constant_values=fill)
    parts = parts.reshape(k, layout.blocks, layout.block)
    parts = jnp.pad(parts, ((0, 0), (0, 0), (0, layout.padded - layout.block)), constant_values=fill)
    return parts.reshape(k, layout.blocks * layout.padded)


def block_coupling(layout, dmat, atoms):
    mine = lax.dynamic_slice_in_dim(atoms, lax.axis_index("ga") * layout.per_shard, layout.per_shard)
    blocks = jnp.take(dmat, mine, axis=0)
    eye = jnp.eye(layout.per_shard, dtype=F32)
    full = (blocks[:, :, None, :] * eye[:, None, :, None]).reshape(layout.used, layout.used)
    extra = layout.rows - layout.used
    return jnp.pad(full, ((0, extra), (0, extra)))


def on_device(psi_k, beta_k, beta_kq, g_k, g_kq, send_index, recv_index, dmat, displaced, mode):
    groups = lax.axis_size("ga")
    total = beta_k.shape[2]
    rows = beta_k.shape[1]
    per_atom = dmat.shape[1]
    layout = Layout(groups, displaced.shape[0], per_atom, total)

    beta_k, beta_kq = jnp.transpose(beta_k, (0, 2, 1)), jnp.transpose(beta_kq, (0, 2, 1))
    if groups == RING * CORE_Y:
        return fused(layout, psi_k, send_index, recv_index, beta_k, beta_kq, displaced, mode, g_k, g_kq, dmat)

    packed = pack_rows(send_index.reshape(1, -1), psi_k)
    arrived = lax.all_to_all(packed, "ga", split_axis=0, concat_axis=0, tiled=True)

    rank = jnp.sum((displaced[None, :] < displaced[:, None]).astype(jnp.int32), axis=1)
    place = rank[None, :] == jnp.arange(displaced.shape[0], dtype=jnp.int32)[:, None]
    atoms = jnp.sum(jnp.where(place, displaced[None, :], 0), axis=1)
    moves = jnp.sum(jnp.where(place[None], mode[:, None, :], 0.0), axis=2)
    steps = jnp.tile(jnp.arange(per_atom, dtype=F32), displaced.shape[0])
    source = jnp.repeat(atoms.astype(F32) * per_atom, per_atom) + steps
    source = pad_rows(layout, source[None], -1.0)
    weights = pad_rows(layout, jnp.repeat(moves, per_atom, axis=1), 0.0)
    filler = jnp.zeros((8 - 1 - weights.shape[0], source.shape[1]), F32)
    info = jnp.concatenate([source, weights, filler], axis=0)
    coupling = block_coupling(layout, dmat, atoms)
    return separate_steps(
        layout, arrived, recv_index.reshape(1, -1), beta_k, beta_kq, info, g_k, g_kq, coupling
    )


def solution(mesh):
    in_specs = (
        P(None, "ga", None),
        P(None, "ga", None),
        P(None, "ga", None),
        P(None, "ga"),
        P(None, "ga"),
        P("ga", None, None),
        P("ga"),
        P(),
        P("pert"),
        P(None, "pert"),
    )
    out_specs = P("pert", "ga", None)
    return jax.shard_map(
        on_device, mesh=mesh, in_specs=in_specs, out_specs=out_specs, check_vma=False
    )
```

profile of v0, /device:TPU:0, one launch (start us, length us, event | category | flops | bytes accessed | tf_op | source)
XLA Modules:
  0.0 78.0 jit_solution(9651422100218940377)
XLA Ops:
  0.0 76.1 %shard_map.136 = bf16[2,512,256]{2,1,0:T(8,128)(2,1)} custom-call(bf16[2,512,256]{2,1,0:T(8,128)(2,1)} %psi_ref.1, s32[16,32]{1,0:T(8,128)} %bitcast.9, s32[1,512]{1,0:T(1,128)} %bitcast.10, s32[1,128]{1,0:T(1,128)} %bitcast.11, f32[3,128]{1,0:T(4,128)} %mode_ref.1, f32[8,2048]{1,0:T(8,128)} %constant.8.clone.table_ref, f32[3,512]{1,0:T(4,128)} %g_k_ref.1, ...), custom_call_target="tpu_custom_call" | custom-call | tf_op jit(solution)/shard_map/pallas_call | solution.py:502
  76.1 1.9 %copy.16 = bf16[2,512,256]{2,1,0:T(8,128)(2,1)} copy(bf16[2,512,256]{2,1,0:T(8,128)(2,1)} %shard_map.136) | data formatting | bytes 1048576
where the time goes:
time: 78.1 us; the launch traced here: 78 us
  Pallas kernels  76.1 us (97%)
  local copies, waits for them, and re-layouts  1.87 us (2%)
    pallas_call x1, Pallas kernels, fused(): pl.pallas_call(functools.partial(fused_kernel, layout), in_specs=[vmem] *...  76.1 us
    unnamed x1, local copies, waits for them, and re-layouts  1.87 us

commit v1 on v0

v1 whole, which is shorter than its diff:
```python
import functools

import jax
import jax.numpy as jnp
import numpy as np
from jax import lax
from jax.experimental import pallas as pl
from jax.experimental.pallas import tpu as pltpu
from jax.sharding import PartitionSpec as P

LANES = 128
RING = 4
CORE_Y = 4
LINE = 4
BLOCKS = 4
COPIES = 120
EARLY = 2
FILL = (5.6, 5.7, 7.8, 10.0)
BF16 = jnp.bfloat16
F32 = jnp.float32
VMEM_LIMIT = 56 * 1024 * 1024


def round_up(value, step):
    return -(-value // step) * step


def dot(a, b):
    return jnp.dot(a, b, preferred_element_type=F32)


def dot_t(a, b):
    return lax.dot_general(a, b, (((0,), (0,)), ((), ())), preferred_element_type=F32)


def pack_kernel(slot_ref, psi_ref, out_ref):
    rows = psi_ref.shape[1]
    bands = psi_ref.shape[2]
    slots = slot_ref.shape[1]
    pick = (lax.broadcasted_iota(jnp.int32, (rows, slots), 0) == slot_ref[...]).astype(BF16)
    for part in range(2):
        out_ref[:, part * bands:(part + 1) * bands] = dot_t(pick, psi_ref[part]).astype(BF16)


def pack_rows(slots, psi_k):
    return pl.pallas_call(
        pack_kernel,
        out_shape=jax.ShapeDtypeStruct((slots.shape[1], 2 * psi_k.shape[2]), BF16),
        compiler_params=pltpu.CompilerParams(vmem_limit_bytes=VMEM_LIMIT),
    )(slots, psi_k)


class Layout:
    def __init__(self, groups, atoms, per_atom, total):
        self.groups = groups
        self.blocks = groups // CORE_Y
        self.gang = CORE_Y
        if self.blocks != RING:
            self.blocks = RING
            self.gang = groups // RING
        self.per_shard = atoms // groups
        self.per_atom = per_atom
        self.used = self.per_shard * per_atom
        self.rows = round_up(self.used, 16)
        self.block = self.gang * self.rows
        self.padded = round_up(self.block, LANES)
        self.total = total
        slack = total - atoms * per_atom
        self.window = min(total, round_up(self.gang * self.used + slack + 16, LANES))
        self.starts = [
            min(b * self.gang * self.used // 16 * 16, total - self.window) for b in range(self.blocks)
        ]


def columns_of(layout, info_ref, b):
    wide = info_ref[:, b * layout.padded:(b + 1) * layout.padded]
    return jnp.transpose(wide)[: layout.block]


def select(layout, beta_ref, info, b):
    start = layout.starts[b]
    ids = lax.broadcasted_iota(jnp.int32, (info.shape[0], layout.window), 1) + start
    pick = (ids == info[:, 0:1].astype(jnp.int32)).astype(BF16)
    rows = pl.ds(start, layout.window)
    return dot(pick, beta_ref[0, rows, :]), dot(pick, beta_ref[1, rows, :])


def row_scale(g_ref, info):
    total = info[:, 1:2] * g_ref[0:1, :]
    for x in range(1, g_ref.shape[0]):
        total = total + info[:, x + 1:x + 2] * g_ref[x:x + 1, :]
    return total


def regroup(arrived_ref, slot_ref, wave):
    slots, rows = arrived_ref.shape[0], wave.shape[0]
    pick = (lax.broadcasted_iota(jnp.int32, (slots, rows), 0) == slot_ref[...]).astype(BF16)
    wave[...] = dot_t(pick, arrived_ref[...]).astype(BF16)


def selected_terms(layout, beta_ref, info, g_ref, b):
    real, imag = select(layout, beta_ref, info, b)
    scale = row_scale(g_ref, info)
    return real, imag, scale * imag, scale * real


def project_block(terms, stacked, store):
    bands = stacked.shape[1] // 2
    x = dot(terms[0], stacked)
    y = dot(terms[1], stacked)
    store(0, (x[:, :bands] + y[:, bands:]).astype(BF16))
    store(1, (x[:, bands:] - y[:, :bands]).astype(BF16))
    x = dot(terms[2], stacked)
    y = dot(terms[3], stacked)
    store(2, (x[:, :bands] - y[:, bands:]).astype(BF16))
    store(3, (x[:, bands:] + y[:, :bands]).astype(BF16))


def prepare_block(layout, beta_ref, info, g_ref, left_ref, b):
    real, imag, slope_real, slope_imag = selected_terms(layout, beta_ref, info, g_ref, b)
    for k, term in enumerate((slope_real, -slope_imag, real, imag)):
        left_ref[b, k] = term.astype(BF16).T


def back_block(left_ref, b, coupled):
    width = coupled.shape[1] // 2
    bands = width // 2
    first, second = coupled[:, :width], coupled[:, width:]
    x = dot(left_ref[b, 0], first) + dot(left_ref[b, 2], second)
    y = dot(left_ref[b, 1], first) + dot(left_ref[b, 3], second)
    return x[:, :bands] - y[:, bands:], x[:, bands:] + y[:, :bands]


def project_kernel(layout, arrived_ref, slot_ref, beta_ref, info_ref, g_ref, out_ref, wave):
    regroup(arrived_ref, slot_ref, wave)
    bands = wave.shape[1] // 2
    for b in range(layout.blocks):

        def store(k, value, b=b):
            out_ref[b * layout.block:(b + 1) * layout.block, k * bands:(k + 1) * bands] = value

        info = columns_of(layout, info_ref, b)
        terms = [term.astype(BF16) for term in selected_terms(layout, beta_ref, info, g_ref, b)]
        project_block(terms, wave[...], store)


def finish_kernel(layout, beta_ref, info_ref, g_ref, coupled_ref, out_ref, left, total):
    for b in range(layout.blocks):
        prepare_block(layout, beta_ref, columns_of(layout, info_ref, b), g_ref, left, b)
        parts = back_block(left, b, coupled_ref[b * layout.block:(b + 1) * layout.block, :])
        for k in range(2):
            total[k] = parts[k] if b == 0 else total[k] + parts[k]
    out_ref[...] = total[...].astype(BF16)


def params(**extra):
    return pltpu.CompilerParams(vmem_limit_bytes=VMEM_LIMIT, **extra)


def separate_steps(layout, arrived, slots, beta_k, beta_kq, info, g_k, g_kq, coupling):
    rows, width = slots.shape[1], arrived.shape[1]
    terms = pl.pallas_call(
        functools.partial(project_kernel, layout),
        out_shape=jax.ShapeDtypeStruct((layout.groups * layout.rows, 2 * width), BF16),
        scratch_shapes=[pltpu.VMEM((rows, width), BF16)],
        compiler_params=params(),
    )(arrived, slots, beta_k, info, g_k)
    shard = lax.psum_scatter(terms.astype(F32), "ga", scatter_dimension=0, tiled=True)
    mixed = jnp.dot(
        coupling, shard, precision=lax.Precision.HIGHEST, preferred_element_type=F32
    ).astype(BF16)
    coupled = lax.all_gather(mixed, "ga", axis=0, tiled=True)
    return pl.pallas_call(
        functools.partial(finish_kernel, layout),
        out_shape=jax.ShapeDtypeStruct((2, rows, width // 2), BF16),
        scratch_shapes=[
            pltpu.VMEM((layout.blocks, 4, rows, layout.block), BF16),
            pltpu.VMEM((2, rows, width // 2), F32),
        ],
        compiler_params=params(),
    )(beta_kq, info, g_kq, coupled)


class Plan:
    def __init__(self, atoms, per_atom, total):
        self.per_atom = per_atom
        self.atoms = atoms // BLOCKS
        self.rows = self.atoms * per_atom
        self.half = self.rows // 2
        slack = total - atoms * per_atom
        self.window = min(total, round_up(self.rows + slack + 16, LANES))
        self.starts = [min(b * self.rows // 16 * 16, total - self.window) for b in range(BLOCKS)]


class Flow:
    def __init__(self, wire, target, device):
        self.k = wire.count
        wire.count += 1
        self.wire, self.target, self.device = wire, target, device

    def copy(self, source):
        return pltpu.make_async_remote_copy(
            src_ref=source,
            dst_ref=self.target,
            send_sem=self.wire.send_sem.at[self.k],
            recv_sem=self.wire.recv_sem.at[self.k],
            device_id={"ga": self.device},
            device_id_type=pl.DeviceIdType.MESH,
        )

    def start(self, source):
        self.copy(source).start()

    def arrived(self):
        self.copy(self.target).wait_recv()

    def sent(self):
        self.copy(self.target).wait_send()


class Wire:
    def __init__(self, send_sem, recv_sem):
        self.send_sem, self.recv_sem, self.count = send_sem, recv_sem, 0


def exact_dot(a, b):
    return jnp.dot(a, b, precision=lax.Precision.HIGHEST, preferred_element_type=F32)


def slot_row(send_ref):
    receivers, cap = send_ref.shape
    column = lax.broadcasted_iota(jnp.int32, (cap, receivers * cap), 1)
    inner = lax.broadcasted_iota(jnp.int32, (cap, receivers * cap), 0)
    wide = exact_dot(send_ref[...].astype(F32), (column % cap == inner).astype(F32))
    column = lax.broadcasted_iota(jnp.int32, wide.shape, 1)
    outer = lax.broadcasted_iota(jnp.int32, wide.shape, 0)
    return jnp.sum(jnp.where(column // cap == outer, wide, 0.0), axis=0, keepdims=True).astype(jnp.int32)


def split_exact(value):
    parts = []
    for _ in range(3):
        parts.append(value.astype(BF16))
        value = value - parts[-1].astype(F32)
    return parts


def divide(index, by):
    return jnp.floor((index.astype(F32) + 0.5) * (1.0 / by))


def sorted_info(plan, displaced_ref, mode_ref, values, info):
    parts = mode_ref.shape[0]
    values[...] = jnp.zeros_like(values)
    values[0:1, :] = displaced_ref[...].astype(F32)
    values[1:1 + parts, :] = mode_ref[...]
    by_atom = jnp.transpose(values[...])
    smaller = (by_atom[:, 0:1] < values[0:1, :]).astype(F32)
    rank = jnp.sum(smaller, axis=0, keepdims=True)
    pieces = split_exact(by_atom)
    row = lax.broadcasted_iota(jnp.int32, (plan.rows, 1), 0)
    slot = divide(row, plan.per_atom)
    proj = row.astype(F32) - slot * plan.per_atom
    lane = lax.broadcasted_iota(jnp.int32, (plan.rows, values.shape[0]), 1)
    for b in range(BLOCKS):
        pick = (slot + float(b * plan.atoms) == rank).astype(BF16)
        found = dot(pick, pieces[0]) + dot(pick, pieces[1]) + dot(pick, pieces[2])
        source = found * plan.per_atom + proj
        info[b] = jnp.where(lane == 0, source, jnp.where(lane == 7, found[:, 0:1], found))


def coupling_matrix(plan, dmat_ref, spread, atom):
    count, step = plan.per_atom, round_up(plan.per_atom, 8)
    spread[...] = jnp.zeros_like(spread)
    for i in range(count):
        spread[i * step:i * step + count, :] = dmat_ref[i]
    row = lax.broadcasted_iota(jnp.int32, (plan.half, 1), 0)
    slot = divide(row, count)
    proj = row.astype(F32) - slot * count
    column = lax.broadcasted_iota(jnp.int32, (1, plan.half), 1)
    column_slot = divide(column, count)
    column_proj = column.astype(F32) - column_slot * count
    lanes = lax.broadcasted_iota(jnp.int32, (plan.half, spread.shape[1]), 1).astype(F32)
    found = lax.dot_general(
        (lanes == atom).astype(F32), spread[...], (((1,), (1,)), ((), ())),
        precision=lax.Precision.HIGHEST, preferred_element_type=F32,
    )
    wide = lax.broadcasted_iota(jnp.int32, (1, count * step), 1)
    found = jnp.where((wide // step).astype(F32) == proj, found, 0.0)
    tall = lax.broadcasted_iota(jnp.int32, (count * step, 1), 0)
    move = ((tall % step).astype(F32) == column_proj).astype(F32)
    return jnp.where(slot == column_slot, exact_dot(found, move), 0.0)


def far_first(n):
    return sorted(range(1, n), key=lambda step: -min(step, n - step))


KINDS = ("A", "B")
UNITS = [("B", q, yy, part) for q in range(1) for yy in range(2) for part in range(2)]
UNITS += [("A", 0, 0, part) for part in range(2)]
UNITS += [("B", 1, yy, part) for yy in range(2) for part in range(2)]
UNITS += [("A", 1, 0, part) for part in range(2)]
SHARES = [(kind, q, part) for q in range(2) for kind in ("A", "O", "P") for part in range(2)]
UNIT = 1.14
HOP = 3.1
COMPUTE = 1.35


def fused_kernel(
    plan, psi_ref, send_ref, slot_ref, displaced_ref, mode_ref, g_k_ref, g_kq_ref, dmat_ref, beta_k_hbm, beta_kq_hbm,
    out_ref, wave, terms, left, mine, y_in, y_sum, side_in, mid_in, yb_in, shared, total, stage, out_in,
    beta_k, beta_kq, packed, arrived, slot_in, g_in, values, info, spread, coupling, send_sem, recv_sem, load_sem,
):
    me = lax.axis_index("ga")
    n = 2 * 2 * LINE
    c, y, z = me % 2, (me // 2) % 2, me // 4
    chip = me // 2
    outer, inner = z % 3 == 0, z % 3 != 0
    is_outer = (2 - z % 3) // 2
    near, far = z // 2, 1 - z // 2

    def index(zz, yy, cc):
        return (zz * 2 + yy) * 2 + cc

    other_core, other_y = index(z, y, 1 - c), index(z, 1 - y, c)
    side, mid = index(z + 1 - 2 * (z % 2), y, c), index(LINE - 1 - z, y, c)
    load_k = pltpu.make_async_copy(beta_k_hbm, beta_k, load_sem.at[0])
    load_k.start()
    load = pltpu.make_async_copy(beta_kq_hbm, beta_kq, load_sem.at[1])
    load.start()

    barrier = pltpu.get_barrier_semaphore()
    for step in range(1, n):
        pl.semaphore_signal(
            barrier, inc=1, device_id={"ga": (me + step) % n}, device_id_type=pl.DeviceIdType.MESH
        )
    rows = psi_ref.shape[1]
    cap = send_ref.shape[1]
    slots = n * cap
    hb = psi_ref.shape[2] // 2
    width = 2 * hb
    half = plan.half
    pick = (lax.broadcasted_iota(jnp.int32, (rows, slots), 0) == slot_row(send_ref)).astype(BF16)
    for part in range(2):
        moved = dot_t(pick, psi_ref[part]).astype(BF16).reshape(n // 2, 2, cap, 2 * hb)
        for cc in range(2):
            packed[:, cc, :, :, part * hb:(part + 1) * hb] = moved[:, :, :, cc * hb:(cc + 1) * hb]
    pl.semaphore_wait(barrier, n - 1)

    wire = Wire(send_sem, recv_sem)

    def flow(target, device):
        return Flow(wire, target, device)

    flows = []
    psi_flows = []
    for step in far_first(n):
        to = (me + step) % n
        psi_flows.append(flow(arrived.at[:, me], to))
        psi_flows[-1].start(packed.at[to // 2, to % 2])
    slot_flow, g_flow = flow(slot_in, other_core), flow(g_in, other_core)
    slot_flow.start(slot_ref)
    g_flow.start(g_k_ref)
    for j in range(2):
        arrived[j, me] = packed[chip, c, j]

    sorted_info(plan, displaced_ref, mode_ref, values, info)
    load_k.wait()
    own_rows, peer_rows = pl.ds(0, rows), pl.ds(rows, rows)
    term_flows = []

    def slopes(b, g_ref, at):
        scale = row_scale(g_ref, info[b])
        terms[b, 2, :, at] = (scale * terms[b, 1, :, at].astype(F32)).astype(BF16)
        terms[b, 3, :, at] = (scale * terms[b, 0, :, at].astype(F32)).astype(BF16)

    for b in range(BLOCKS):
        for k, value in enumerate(select(plan, beta_k, info[b], b)):
            terms[b, k, :, own_rows] = value.astype(BF16)
        term_flows.append(flow(terms.at[b, pl.ds(0, 2), :, peer_rows], other_core))
        term_flows[b].start(terms.at[b, pl.ds(0, 2), :, own_rows])
        slopes(b, g_k_ref, own_rows)
        if b == 0:
            g_flow.arrived()
        else:
            term_flows[b - 1].arrived()
            slopes(b - 1, g_in, peer_rows)
    term_flows[BLOCKS - 1].arrived()
    slopes(BLOCKS - 1, g_in, peer_rows)

    left_flows = []

    def prepare(b):
        if b == 0:
            load.wait()
        real, imag = select(plan, beta_kq, info[b], b)
        scale = row_scale(g_kq_ref, info[b])
        for k, term in enumerate((scale * imag, -(scale * real), real, imag)):
            left[b, k, own_rows] = term.astype(BF16).T
        left_flows.append(flow(left.at[b, :, peer_rows], other_core))
        left_flows[b].start(left.at[b, :, own_rows])

    for b in range(EARLY):
        prepare(b)

    slot_flow.arrived()
    for copy in psi_flows:
        copy.arrived()
    for h, ref, owner in ((0, slot_ref, c), (1, slot_in, 1 - c)):
        pick = (lax.broadcasted_iota(jnp.int32, (slots, rows), 0) == ref[...]).astype(BF16)
        wave[h * rows:(h + 1) * rows] = dot_t(pick, arrived[owner].reshape(slots, width)).astype(BF16)

    order = (2 * far, 2 * far + 1, 2 * near, 2 * near + 1)
    ya = [flow(y_in.at[i], other_y) for i in range(BLOCKS)]
    rs_side = [flow(side_in.at[k], side) for k in range(len(UNITS))]
    rs_mid = [flow(mid_in.at[k], mid) for k in range(len(UNITS))]
    yb = [[flow(yb_in.at[q, part], other_y) for part in range(2)] for q in range(2)]

    def spot(h, kind, q, part):
        base = 0 if kind == "A" else width
        yy = 1 - y if kind == "P" else y
        return shared.at[2 * h + q, yy, :, pl.ds(base + part * hb, hb)]

    yg = [[flow(spot(near, "O", q, part), other_y) for part in range(2)] for q in range(2)]
    ga_y = [
        [[flow(spot(h, "A", q, part), other_y) for part in range(2)] for q in range(2)] for h in (near, far)
    ]
    out_h = z % 2
    ag_side = [flow(spot(out_h, *share), side) for share in SHARES]
    ag_side_in = [spot(1 - out_h, *share) for share in SHARES]
    ag_mid = [flow(spot(near, *share), mid) for share in SHARES]

    def own_unit(k, h, ysum_at):
        kind, q, yy, part = UNITS[k]
        if kind == "A":
            return y_sum[ysum_at + q, :, part * hb:(part + 1) * hb].astype(F32)
        return mine[2 * h + q, yy, :, width + part * hb:width + (part + 1) * hb].astype(F32)

    def project(i):
        b = order[i]
        x = dot(terms[b, 0], wave[...])
        v = dot(terms[b, 1], wave[...])

        def store(at, value):
            for yy in range(2):
                mine[b, yy, :, at:at + hb] = value[yy * half:(yy + 1) * half].astype(BF16)

        store(0, x[:, :hb] + v[:, hb:])
        store(hb, x[:, hb:] - v[:, :hb])
        ya[i].start(mine.at[b, 1 - y, :, pl.ds(0, width)])
        x = dot(terms[b, 2], wave[...])
        v = dot(terms[b, 3], wave[...])
        store(2 * hb, x[:, :hb] - v[:, hb:])
        store(3 * hb, x[:, hb:] + v[:, :hb])

    def head(kind, q):
        for k, unit in enumerate(UNITS):
            if unit[0] != kind or unit[1] != q:
                continue
            if kind == "A":
                rs_side[k].start(y_sum.at[q, :, pl.ds(unit[3] * hb, hb)])
            else:
                rs_side[k].start(mine.at[2 * far + q, unit[2], :, pl.ds(width + unit[3] * hb, hb)])

    def settle_y(i):
        ya[i].arrived()
        y_sum[i] = (mine[order[i], y, :, :width].astype(F32) + y_in[i].astype(F32)).astype(BF16)

    def inner_side(k):
        rs_side[k].arrived()
        side_in[k] = (side_in[k].astype(F32) + own_unit(k, far, 0)).astype(BF16)
        rs_mid[k].start(side_in.at[k])

    def inner_mid(k):
        rs_mid[k].arrived()
        mid_in[k] = (mid_in[k].astype(F32) + own_unit(k, near, 2)).astype(BF16)
        rs_side[k].start(mid_in.at[k])

    def couple(q, value):
        return exact_dot(coupling[q], value).astype(BF16)

    def share_at(kind, q, part):
        return SHARES.index((kind, q, part))

    def outer_side(k):
        kind, q, yy, part = UNITS[k]
        rs_side[k].arrived()
        value = side_in[k].astype(F32) + own_unit(k, near, 2)
        if kind == "A":
            spot(near, "A", q, part)[...] = couple(q, value)
            ag_side[share_at("A", q, part)].start(spot(near, "A", q, part))
            ga_y[0][q][part].start(spot(near, "A", q, part))
        else:
            side_in[k] = value.astype(BF16)

    def first_unit(q):
        return UNITS.index(("B", q, 0, 0))

    def outer_swap(q):
        for part in range(2):
            yb[q][part].start(side_in.at[first_unit(q) + 2 * (1 - y) + part])

    def outer_couple(q, part):
        yb[q][part].arrived()
        value = side_in[first_unit(q) + 2 * y + part].astype(F32) + yb_in[q, part].astype(F32)
        spot(near, "O", q, part)[...] = couple(q, value)
        yg[q][part].start(spot(near, "O", q, part))
        ag_side[share_at("O", q, part)].start(spot(near, "O", q, part))

    def outer_pass(q, part):
        yg[q][part].arrived()
        ag_side[share_at("P", q, part)].start(spot(near, "P", q, part))

    def inner_ag_side(k):
        kind, q, part = SHARES[k]
        ag_side[k].arrived()
        ag_mid[k].start(spot(near, *SHARES[k]))
        if kind == "A":
            ga_y[0][q][part].start(spot(near, *SHARES[k]))

    def inner_ag_mid(k):
        kind, q, part = SHARES[k]
        ag_mid[k].arrived()
        ag_side[k].start(spot(far, *SHARES[k]))
        if kind == "A":
            ga_y[1][q][part].start(spot(far, *SHARES[k]))

    def outer_ag(k):
        kind, q, part = SHARES[k]
        ag_side[k].arrived()
        if kind == "A":
            ga_y[1][q][part].start(spot(far, *SHARES[k]))

    done_left = set()

    def back(h, q, kind):
        which = (near, far)[h]
        if h == 0 and q == 0 and kind == "A":
            for copy in left_flows:
                copy.arrived()
        if kind == "A":
            for part in range(2):
                ga_y[h][q][part].arrived()
        b = 2 * which + q
        base, at = (0, 0) if kind == "A" else (width, 2)
        value = shared[b, :, :, base:base + width].reshape(plan.rows, width)
        x = dot(left[b, at], value)
        v = dot(left[b, at + 1], value)
        first = h == 0 and q == 0 and kind == "A"
        for part, term in ((0, x[:, :hb] - v[:, hb:]), (1, x[:, hb:] + v[:, :hb])):
            total[part] = term if first else total[part] + term

    def make_coupling():
        for q in range(2):
            atom = info[2 * near + q, pl.ds(pl.multiple_of(y * half, 8), half), 7:8]
            coupling[q] = coupling_matrix(plan, dmat_ref, spread, atom)

    events = schedule(
        project, head, settle_y, inner_side, inner_mid, outer_side, outer_swap, outer_couple, outer_pass,
        inner_ag_side, inner_ag_mid, outer_ag, back, make_coupling, prepare,
    )
    role_now, batch = None, []

    def flush():
        if not batch:
            return
        todo = list(batch)
        batch.clear()

        def run():
            for f, args in todo:
                f(*args)

        if role_now == "all":
            run()
        else:
            pl.when(outer if role_now == "outer" else inner)(run)

    for role, f, args in events:
        if role != role_now:
            flush()
            role_now = role
        batch.append((f, args))
    flush()

    out_flow = flow(out_in, other_core)
    for part in range(2):
        stage[part] = total[part, peer_rows].astype(BF16)
    out_flow.start(stage)
    for part in range(2):
        out_ref[part, :, pl.ds(pl.multiple_of(c * hb, hb), hb)] = total[part, own_rows].astype(BF16)
    out_flow.arrived()
    for part in range(2):
        out_ref[part, :, pl.ds(pl.multiple_of((1 - c) * hb, hb), hb)] = out_in[part]

    everyone = psi_flows + [slot_flow, g_flow, out_flow] + term_flows + left_flows + ya + rs_side + ag_side
    for pairs in ga_y:
        for pair in pairs:
            everyone += pair
    for copy in everyone:
        copy.sent()

    @pl.when(inner)
    def _():
        for copy in rs_mid + ag_mid:
            copy.sent()

    @pl.when(outer)
    def _():
        for pair in yb + yg:
            for copy in pair:
                copy.sent()


def schedule(
    project, head, settle_y, inner_side, inner_mid, outer_side, outer_swap, outer_couple, outer_pass,
    inner_ag_side, inner_ag_mid, outer_ag, back, make_coupling, prepare,
):
    events = []

    def at(time, role, f, *args):
        events.append((time, len(events), role, f, args))

    ready = COMPUTE * BLOCKS
    for i in range(BLOCKS):
        at(COMPUTE * i, "all", project, i)
        if i == 0:
            at(COMPUTE * i + 0.1, "outer", head, "B", 0)
    for i in range(BLOCKS):
        time = max(ready, COMPUTE + (i + 1) * 2 * UNIT + 2.0) + 0.01
        at(time, "all", settle_y, i)
        if i == 0:
            at(time + 0.001, "outer", head, "A", 0)
            at(time + 0.002, "outer", head, "B", 1)
        if i == 1:
            at(time + 0.001, "outer", head, "A", 1)
    settled = [max(ready, COMPUTE + (i + 1) * 2 * UNIT + 2.0) for i in range(BLOCKS)]

    def own_ready(k, i):
        return settled[i + UNITS[k][1]] if UNITS[k][0] == "A" else 0.0

    last_side, last_mid, last_out = 0.0, 0.0, 0.0
    out_time = []
    for k in range(len(UNITS)):
        last_side = max(COMPUTE + 2.0 + UNIT * (k + 1), last_side + UNIT, own_ready(k, 0) + 0.02)
        at(last_side, "inner", inner_side, k)
        last_mid = max(last_side + HOP, last_mid + UNIT, own_ready(k, 2) + 0.02)
        at(last_mid, "inner", inner_mid, k)
        last_out = max(last_mid + HOP, last_out + UNIT, own_ready(k, 2) + 0.02)
        at(last_out, "outer", outer_side, k)
        out_time.append(last_out)
    starts = {}
    for q in range(2):
        for part in range(2):
            k = UNITS.index(("A", q, 0, part))
            starts[("A", q, part)] = out_time[k] + 0.3
        swapped = out_time[UNITS.index(("B", q, 1, 1))] + 0.05
        at(swapped, "outer", outer_swap, q)
        for part in range(2):
            time = swapped + 2.0 + UNIT * (part + 1)
            at(time, "outer", outer_couple, q, part)
            starts[("O", q, part)] = time + 0.3
            at(time + HOP + 0.3, "outer", outer_pass, q, part)
            starts[("P", q, part)] = time + HOP + 0.4
    free = 0.0
    ready_at = {}
    for share in sorted(SHARES, key=lambda share: starts[share]):
        k = SHARES.index(share)
        free = max(free, starts[share]) + UNIT
        times = [free + 2.0, free + 2.0 + HOP, free + 2.0 + 2 * HOP]
        at(times[0], "inner", inner_ag_side, k)
        at(times[1], "inner", inner_ag_mid, k)
        at(times[2], "outer", outer_ag, k)
        ready_at[share] = (times[0], times[2])
    for h in range(2):
        for q in range(2):
            for kind in ("A", "B"):
                names = ("A",) if kind == "A" else ("O", "P")
                time = max(ready_at[(name, q, part)][h] for name in names for part in range(2))
                at(time + (HOP if kind == "A" else 0.0) + 0.01 * h, "all", back, h, q, kind)
    at(FILL[0], "outer", make_coupling)
    for b in range(EARLY, BLOCKS):
        at(FILL[b], "all", prepare, b)
    order = sorted(events, key=lambda event: event[:2])
    backs = [event for event in order if event[3] is back]
    first = next(event for event in backs if event[4] == (0, 0, "A"))
    if backs[0] is not first:
        place = order.index(backs[0])
        order.remove(first)
        order.insert(place, first)
    return [(role, f, args) for _, _, role, f, args in order]


def fused(plan, psi_k, send_index, recv_index, beta_k, beta_kq, displaced, mode, g_k, g_kq, dmat):
    rows, bands = psi_k.shape[1:]
    hb = bands // 2
    groups, cap = send_index.shape[1:]
    half = plan.half
    vmem = pl.BlockSpec(memory_space=pltpu.VMEM)
    units = len(UNITS)

    def buffer(*shape, dtype=BF16):
        return pltpu.VMEM(shape, dtype)

    return pl.pallas_call(
        functools.partial(fused_kernel, plan),
        in_specs=[vmem] * 8 + [pl.BlockSpec(memory_space=pl.ANY)] * 2,
        out_specs=vmem,
        out_shape=jax.ShapeDtypeStruct((2, rows, bands), BF16),
        scratch_shapes=[
            buffer(2 * rows, bands),
            buffer(BLOCKS, 4, plan.rows, 2 * rows),
            buffer(BLOCKS, 4, 2 * rows, plan.rows),
            buffer(BLOCKS, 2, half, 2 * bands),
            buffer(BLOCKS, half, bands),
            buffer(BLOCKS, half, bands),
            buffer(units, half, hb),
            buffer(units, half, hb),
            buffer(2, 2, half, hb),
            buffer(BLOCKS, 2, half, 2 * bands),
            buffer(2, 2 * rows, hb, dtype=F32),
            buffer(2, rows, hb),
            buffer(2, rows, hb),
            pltpu.VMEM(beta_k.shape, BF16),
            pltpu.VMEM(beta_kq.shape, BF16),
            buffer(groups // 2, 2, 2, cap, bands),
            buffer(2, groups, cap, bands),
            buffer(1, rows, dtype=jnp.int32),
            buffer(*g_k.shape, dtype=F32),
            buffer(8, displaced.shape[0], dtype=F32),
            buffer(BLOCKS, plan.rows, 8, dtype=F32),
            buffer(plan.per_atom * round_up(plan.per_atom, 8), dmat.shape[0], dtype=F32),
            buffer(2, half, half, dtype=F32),
            pltpu.SemaphoreType.DMA((COPIES,)),
            pltpu.SemaphoreType.DMA((COPIES,)),
            pltpu.SemaphoreType.DMA((2,)),
        ],
        compiler_params=params(collective_id=0, has_side_effects=True),
    )(
        psi_k, send_index[0], recv_index.reshape(1, -1), displaced.reshape(1, -1), mode, g_k, g_kq,
        jnp.transpose(dmat, (1, 2, 0)), beta_k, beta_kq,
    )


def pad_rows(layout, values, fill):
    k = values.shape[0]
    parts = values.reshape(k, layout.groups, layout.used)
    parts = jnp.pad(parts, ((0, 0), (0, 0), (0, layout.rows - layout.used)), constant_values=fill)
    parts = parts.reshape(k, layout.blocks, layout.block)
    parts = jnp.pad(parts, ((0, 0), (0, 0), (0, layout.padded - layout.block)), constant_values=fill)
    return parts.reshape(k, layout.blocks * layout.padded)


def block_coupling(layout, dmat, atoms):
    mine = lax.dynamic_slice_in_dim(atoms, lax.axis_index("ga") * layout.per_shard, layout.per_shard)
    blocks = jnp.take(dmat, mine, axis=0)
    eye = jnp.eye(layout.per_shard, dtype=F32)
    full = (blocks[:, :, None, :] * eye[:, None, :, None]).reshape(layout.used, layout.used)
    extra = layout.rows - layout.used
    return jnp.pad(full, ((0, extra), (0, extra)))


def on_device(psi_k, beta_k, beta_kq, g_k, g_kq, send_index, recv_index, dmat, displaced, mode):
    groups = lax.axis_size("ga")
    total = beta_k.shape[2]
    rows = beta_k.shape[1]
    per_atom = dmat.shape[1]
    beta_k, beta_kq = jnp.transpose(beta_k, (0, 2, 1)), jnp.transpose(beta_kq, (0, 2, 1))
    if groups == 4 * LINE:
        plan = Plan(displaced.shape[0], per_atom, total)
        return fused(plan, psi_k, send_index, recv_index, beta_k, beta_kq, displaced, mode, g_k, g_kq, dmat)

    layout = Layout(groups, displaced.shape[0], per_atom, total)

    packed = pack_rows(send_index.reshape(1, -1), psi_k)
    arrived = lax.all_to_all(packed, "ga", split_axis=0, concat_axis=0, tiled=True)

    rank = jnp.sum((displaced[None, :] < displaced[:, None]).astype(jnp.int32), axis=1)
    place = rank[None, :] == jnp.arange(displaced.shape[0], dtype=jnp.int32)[:, None]
    atoms = jnp.sum(jnp.where(place, displaced[None, :], 0), axis=1)
    moves = jnp.sum(jnp.where(place[None], mode[:, None, :], 0.0), axis=2)
    steps = jnp.tile(jnp.arange(per_atom, dtype=F32), displaced.shape[0])
    source = jnp.repeat(atoms.astype(F32) * per_atom, per_atom) + steps
    source = pad_rows(layout, source[None], -1.0)
    weights = pad_rows(layout, jnp.repeat(moves, per_atom, axis=1), 0.0)
    filler = jnp.zeros((8 - 1 - weights.shape[0], source.shape[1]), F32)
    info = jnp.concatenate([source, weights, filler], axis=0)
    coupling = block_coupling(layout, dmat, atoms)
    return separate_steps(
        layout, arrived, recv_index.reshape(1, -1), beta_k, beta_kq, info, g_k, g_kq, coupling
    )


def solution(mesh):
    in_specs = (
        P(None, "ga", None),
        P(None, "ga", None),
        P(None, "ga", None),
        P(None, "ga"),
        P(None, "ga"),
        P("ga", None, None),
        P("ga"),
        P(),
        P("pert"),
        P(None, "pert"),
    )
    out_specs = P("pert", "ga", None)
    return jax.shard_map(
        on_device, mesh=mesh, in_specs=in_specs, out_specs=out_specs, check_vma=False
    )
```

time: 78.1 us -> 69.8 us (0.89)
  Pallas kernels: 76.1 us -> 67.7 us
    pallas_call x1, Pallas kernels: 76.1 us -> 67.7 us  [fused(): pl.pallas_call(functools.partial(fused_kernel, plan), in_specs=[vmem] * 8...]
where the time goes in v1:
time: 69.8 us; the launch traced here: 69.6 us
  Pallas kernels  67.7 us (97%)
  local copies, waits for them, and re-layouts  1.87 us (3%)
    pallas_call x1, Pallas kernels, fused(): pl.pallas_call(functools.partial(fused_kernel, plan), in_specs=[vmem] * 8...  67.7 us
    unnamed x1, local copies, waits for them, and re-layouts  1.87 us

profile of v1, /device:TPU:0, one launch (start us, length us, event | category | flops | bytes accessed | tf_op | source)
XLA Modules:
  0.0 69.6 jit_solution(17060237298583159874)
XLA Ops:
  0.0 67.7 %shard_map.100 = bf16[2,512,256]{2,1,0:T(8,128)(2,1)} custom-call(bf16[2,512,256]{2,1,0:T(8,128)(2,1)} %psi_ref.1, s32[16,32]{1,0:T(8,128)} %bitcast.9, s32[1,512]{1,0:T(1,128)} %bitcast.10, s32[1,128]{1,0:T(1,128)} %bitcast.11, f32[3,128]{1,0:T(4,128)} %mode_ref.1, f32[3,512]{1,0:T(4,128)} %g_k_ref.1, f32[3,512]{1,0:T(4,128)} %g_kq_ref.1, ...), custom_call_target="tpu_custom_call" | custom-call | tf_op jit(solution)/shard_map/pallas_call | solution.py:706
  67.7 1.9 %copy.12 = bf16[2,512,256]{2,1,0:T(8,128)(2,1)} copy(bf16[2,512,256]{2,1,0:T(8,128)(2,1)} %shard_map.100) | data formatting | bytes 1048576
